TPU v7x, 64 devices: a 2x2x8 block of a 4x4x8 slice. The times are simulated.
64 devices in a mesh: dp: 4 (over x, y), sp: 16 (over z, core).
Axes of the slice: x: 2, y: 2, z: 8, core: 2. Of those that a mesh axis runs over, the one named last changes fastest.
The devices are a block of a 4x4x8 slice.
Arguments:
- hidden: bfloat16 [64, 512, 2048], P('dp', 'sp'), parts along dimension 0
- pos_ids: int32 [64, 512], P('dp', 'sp'), parts along dimension 0
- block_ids: int32 [64, 512], P('dp', 'sp'), parts along dimension 0
- ctx_len: int32 [64], P('dp'), parts along dimension 0
- ln_gamma: bfloat16 [2048], replicated
- ln_beta: bfloat16 [2048], replicated
- w_qkv: bfloat16 [2048, 32, 3, 64], replicated
- b_qkv: bfloat16 [32, 3, 64], replicated
- w_dense: bfloat16 [2048, 2048], replicated
- b_dense: bfloat16 [2048], replicated
Outputs:
- output 1: bfloat16 [64, 512, 2048], P('dp', 'sp'), parts along dimension 0
- output 2: bfloat16 [64, 512, 32, 64], P('dp', None, 'sp'), parts along dimension 0
- output 3: bfloat16 [64, 512, 32, 64], P('dp', None, 'sp'), parts along dimension 0
There are 4 independent parts. A program takes and returns all parts, laid end to end along the dimension named above; an argument that names none is the same for every part.
All inputs are finite; a program needn't handle non-finite values.
Results may differ from a plain program's by a relative error of at most 0.00608031.
Values are sent between devices in bfloat16 or wider.
A program may use at most 768 MiB of HBM per device.

v0:
```python
import math
import jax
import jax.numpy as jnp
from jax import lax
from jax.sharding import PartitionSpec as P

ALPHA = math.sqrt(56.0)
ROPE_BASE = 10000.0
LN_EPS = 1e-5
SCORE_BUDGET = 2 ** 25


def layer_norm(hidden, ln_gamma, ln_beta):
    wide_in = hidden.astype(jnp.float32)
    row_mean = jnp.mean(wide_in, axis=-1, keepdims=True)
    centered = wide_in - row_mean
    row_var = jnp.mean(jnp.square(centered), axis=-1, keepdims=True)
    return (centered * lax.rsqrt(row_var + LN_EPS) * ln_gamma.astype(jnp.float32) + ln_beta.astype(jnp.float32)).astype(jnp.bfloat16)


def rotate_pairs(qk_pair, pos_ids, block_ids):
    half_dim = qk_pair.shape[-1] // 2
    quarter_dim = half_dim // 2
    inv_freq = ROPE_BASE ** (-jnp.arange(0, half_dim, 2).astype(jnp.float32) / half_dim)
    angles = jnp.stack([pos_ids, block_ids], axis=-1).astype(jnp.float32)[..., None] * inv_freq
    cos_a = jnp.cos(angles)[:, :, None, None]
    sin_a = jnp.sin(angles)[:, :, None, None]
    split_dims = qk_pair.astype(jnp.float32).reshape(qk_pair.shape[:-1] + (2, 2, quarter_dim))
    low_part = split_dims[..., 0, :]
    high_part = split_dims[..., 1, :]
    new_low = low_part * cos_a - high_part * sin_a
    new_high = high_part * cos_a + low_part * sin_a
    return jnp.stack([new_low, new_high], axis=-2).reshape(qk_pair.shape).astype(jnp.bfloat16)


def query_block(cell_count, query_len, key_len):
    block_len = query_len
    while block_len % 2 == 0 and block_len > 8 and cell_count * block_len * key_len > SCORE_BUDGET:
        block_len = block_len // 2
    return block_len


def attend(query_rot, key_heads, value_heads, ctx_len, q_offset):
    row_count, query_len, head_count, head_dim = query_rot.shape
    key_len = key_heads.shape[1]
    block_len = query_block(row_count * head_count, query_len, key_len)
    score_scale = 1.0 / math.sqrt(head_dim)
    key_pos = jnp.arange(key_len)
    ctx_visible = (key_pos[None, :] < ctx_len[:, None])[:, None, None, :]

    def attend_block(block_idx, context):
        block_start = block_idx * block_len
        q_block = lax.dynamic_slice_in_dim(query_rot, block_start, block_len, axis=1)
        scores = jnp.einsum('bqhe,bkhe->bhqk', q_block, key_heads, preferred_element_type=jnp.float32) * score_scale
        q_pos = q_offset + block_start + jnp.arange(block_len)
        visible = ctx_visible | (key_pos[None, None, None, :] <= q_pos[None, None, :, None])
        attn_probs = jax.nn.softmax(jnp.where(visible, scores, -jnp.inf), axis=-1).astype(jnp.bfloat16)
        block_out = jnp.einsum('bhqk,bkhe->bqhe', attn_probs, value_heads, preferred_element_type=jnp.float32).astype(jnp.bfloat16)
        return lax.dynamic_update_slice_in_dim(context, block_out, block_start, axis=1)

    return lax.fori_loop(0, query_len // block_len, attend_block, jnp.zeros_like(query_rot))


def solution(mesh):
    seq_spec = P('dp', 'sp', None)
    row_spec = P('dp', 'sp')
    head_spec = P('dp', None, 'sp', None)
    replicated = P()

    def local_block(hidden, pos_ids, block_ids, ctx_len, ln_gamma, ln_beta, w_qkv, b_qkv, w_dense, b_dense):
        normed = layer_norm(hidden, ln_gamma, ln_beta)
        qkv_proj = (jnp.einsum('bsd,dhte->bshte', normed, w_qkv, preferred_element_type=jnp.float32) + b_qkv.astype(jnp.float32)).astype(jnp.bfloat16)
        qk_rot = rotate_pairs(qkv_proj[:, :, :, :2], pos_ids, block_ids)
        qkv_rot = jnp.concatenate([qk_rot, qkv_proj[:, :, :, 2:]], axis=3)
        by_heads = lax.all_to_all(qkv_rot, 'sp', 2, 1, tiled=True)
        key_heads = by_heads[:, :, :, 1]
        value_heads = by_heads[:, :, :, 2]
        context = attend(by_heads[:, :, :, 0], key_heads, value_heads, ctx_len, 0)
        by_tokens = lax.all_to_all(context, 'sp', 1, 2, tiled=True)
        head_count, head_dim = by_tokens.shape[2], by_tokens.shape[3]
        dense_out = jnp.einsum('bshe,hef->bsf', by_tokens, w_dense.reshape(head_count, head_dim, -1), preferred_element_type=jnp.float32)
        block_out = (normed.astype(jnp.float32) * ALPHA + dense_out + b_dense.astype(jnp.float32)).astype(jnp.bfloat16)
        return block_out, key_heads, value_heads

    return jax.shard_map(local_block, mesh=mesh, in_specs=(seq_spec, row_spec, row_spec, P('dp'), replicated, replicated, replicated, replicated, replicated, replicated), out_specs=(seq_spec, head_spec, head_spec), check_vma=False)
```

profile of v0, /device:TPU:21, one launch (start us, length us, event | category | flops | bytes accessed | tf_op | source)
XLA Modules:
  0.0 517.2 jit_solution(17959495895303864909)
XLA Ops:
  0.6 1.9 convert_reduce_fusion
  2.6 2.3 fusion.12
  4.9 0.7 convert_element_type.58
  5.6 0.7 convert_element_type.59
  6.3 0.8 copy.29
  7.0 0.0 copy-done.1
  7.1 0.0 copy-done.7
  7.1 0.0 copy-done.3
  7.1 0.0 copy-done.5
  7.1 31.7 %add_convert_fusion = bf16[16,32,32,3,64]{4,1,3,2,0:T(8,128)(2,1)} fusion(f32[32,3,64]{2,1,0:T(4,128)S(1)} %copy.29, bf16[2048,32,3,64]{0,3,2,1:T(8,128)(2,1)} %param.16, bf16[16,32,2048]{2,1,0:T(8,128)(2,1)} %param.10, f32[2048]{0:T(1024)S(1)} %convert_element_type.59, f32[2048]{0:T(1024)S(1)} %convert_element_type.58, f32[16,32]{1,0:T(8,128)S(1)} %add_rsqrt_fusion, ...), kind=kOutput, calls=%fused_computation.8 | convolution fusion | flops 12897484800 | bytes 33599488 | tf_op jit(solution)/shard_map/bsd,dhte->bshte/dot_general | solution.py:72
  38.8 11.5 %slice_convert_fusion = f32[16,32,32,2,64]{4,1,3,2,0:T(8,128)} fusion(bf16[16,32,32,3,64]{4,1,3,2,0:T(8,128)(2,1)} %add_convert_fusion), kind=kLoop, calls=%fused_computation.16 | loop fusion | flops 2097152 | bytes 12582912 | tf_op jit(solution)/shard_map/reshape | solution.py:28
  50.3 5.2 %slice.31 = bf16[16,32,32,1,64]{4,1,3,2,0:T(8,128)(2,1)} slice(bf16[16,32,32,3,64]{4,1,3,2,0:T(8,128)(2,1)} %add_convert_fusion), slice={[0:16], [0:32], [0:32], [2:3], [0:64]} | slice | bytes 4194304 | tf_op jit(solution)/shard_map/slice | solution.py:74
  55.5 24.0 %copy.30 = f32[16,32,32,2,64]{2,4,3,1,0:T(8,128)} copy(f32[16,32,32,2,64]{4,1,3,2,0:T(8,128)} %slice_convert_fusion) | data formatting | bytes 16777216 | tf_op jit(solution)/shard_map/reshape | solution.py:28
  79.5 0.2 copy.31
  79.7 9.4 %copy.32 = bf16[16,32,32,1,64]{2,4,3,1,0:T(8,128)(2,1)} copy(bf16[16,32,32,1,64]{4,1,3,2,0:T(8,128)(2,1)} %slice.31) | data formatting | bytes 4194304 | tf_op jit(solution)/shard_map/slice | solution.py:74
  89.1 7.9 %multiply_cosine_fusion = (f32[16,32,2,16]{3,2,1,0:T(2,128)S(1)}, f32[16,32,2,16]{3,2,1,0:T(2,128)S(1)}) fusion(f32[16]{0:T(128)S(1)} %multiply_power_fusion, f32[16,32,2]{2,1,0:T(8,128)S(1)} %copy.31), kind=kLoop, calls=%fused_computation.37 | loop fusion | flops 16384 | bytes 135232 | tf_op jit(solution)/shard_map/cos | solution.py:26
  97.1 0.0 slice-start.1
  97.1 12.1 %subtract_convert_fusion = (bf16[16,32,32,2,2,1,16]{2,6,5,4,3,1,0:T(8,128)(2,1)S(1)}, bf16[16,32,32,2,2,1,16]{2,6,5,4,3,1,0:T(8,128)(2,1)S(1)}) fusion(f32[16,32,32,2,2,2,16]{2,6,5,4,3,1,0:T(8,128)} %bitcast.57, f32[16,32,2,16]{3,2,1,0:T(2,128)S(1)} %get-tuple-element.32, f32[16,32,2,16]{3,2,1,0:T(2,128)S(1)} %get-tuple-element.23), kind=kLoop, calls=%fused_computation.13 | loop fusion | flops 8388608 | bytes 12713984 | tf_op jit(solution)/shard_map/convert.1
  109.2 3.4 pad_maximum_fusion.1
  112.6 0.0 slice-done
  112.6 0.0 slice-done.1
  112.6 15.7 %pad_maximum_fusion = bf16[16,32,32,3,64]{2,4,3,1,0:T(8,128)(2,1)} fusion(bf16[16,32,32,1,64]{2,4,3,1,0:T(8,128)(2,1)S(1)} %bitcast.65, bf16[16,32,32,2,64]{2,4,3,1,0:T(8,128)(2,1)S(1)} %bitcast.61), kind=kLoop, calls=%fused_computation.5 | loop fusion | flops 3145728 | bytes 12582912 | tf_op jit(solution)/shard_map/concatenate | solution.py:74
  128.3 29.6 %copy.33 = bf16[16,32,32,3,64]{4,1,3,0,2:T(8,128)(2,1)} copy(bf16[16,32,32,3,64]{2,4,3,1,0:T(8,128)(2,1)} %pad_maximum_fusion) | data formatting | bytes 12582912 | tf_op jit(solution)/shard_map/concatenate | solution.py:74
  157.9 16.7 %reshape.111 = bf16[16,2,98304]{2,1,0:T(2,128)(2,1)} reshape(bf16[32,16,3,32,64]{4,3,2,1,0:T(8,128)(2,1)} %bitcast.63) | data formatting | bytes 12582912
  174.6 10.9 %all-to-all-start = ((bf16[16,2,98304]{2,1,0:T(2,128)(2,1)}), bf16[16,2,98304]{2,1,0:T(2,128)(2,1)}, u32[]{:S(2)}, u32[]{:S(2)}) async-start(bf16[16,2,98304]{2,1,0:T(2,128)(2,1)} %reshape.111), calls=%async_computation | async-start | bytes 12582912 | tf_op jit(solution)/shard_map/all_to_all | solution.py:75
  185.5 0.1 iota_compare_fusion
  185.6 0.0 copy-done.12
  185.6 0.1 iota_compare_fusion.1
  185.7 3.7 broadcast_or_fusion
  189.3 137.4 %all-to-all-done = bf16[16,2,98304]{2,1,0:T(2,128)(2,1)} async-done(((bf16[16,2,98304]{2,1,0:T(2,128)(2,1)}), bf16[16,2,98304]{2,1,0:T(2,128)(2,1)}, u32[]{:S(2)}, u32[]{:S(2)}) %all-to-all-start) | async-done | bytes 6291488 | tf_op jit(solution)/shard_map/all_to_all | solution.py:75
  326.7 16.3 %reshape.112 = bf16[32,16,3,32,64]{4,3,2,1,0:T(8,128)(2,1)} reshape(bf16[16,2,98304]{2,1,0:T(2,128)(2,1)} %all-to-all-done) | data formatting | bytes 12582912
  343.0 11.6 %copy.35 = bf16[16,16,32,2,3,64]{5,2,1,4,3,0:T(8,128)(2,1)} copy(bf16[16,16,32,2,3,64]{5,2,4,0,3,1:T(8,128)(2,1)} %bitcast.62) | data formatting | bytes 12582912 | tf_op jit(solution)/shard_map/all_to_all | solution.py:75
  354.6 19.1 %fusion.16 = f32[16,2,512,512]{2,3,1,0:T(8,128)} fusion(bf16[16,512,2,3,64]{4,1,3,2,0:T(8,128)(2,1)} %bitcast.58), kind=kOutput, calls=%fused_computation.27 | convolution fusion | flops 1073741824 | bytes 41943040 | tf_op jit(solution)/shard_map/while/body/eval_jaxpr/bqhe,bkhe->bhqk/dot_general | solution.py:54
  373.7 37.1 %fusion.30 = (f32[16,2,512]{2,1,0:T(2,128)S(1)}, f32[16,2,512,512]{2,3,1,0:T(8,128)}) fusion(f32[16,2,512,512]{2,3,1,0:T(8,128)} %fusion.16, pred[16,512,512]{1,2,0:T(8,128)(4,1)} %broadcast_or_fusion), kind=kOutput, calls=%fused_computation.48 | output fusion | flops 50332160 | bytes 71368704 | tf_op jit(solution)/shard_map/while/body/eval_jaxpr/sub | solution.py:57
  410.8 13.4 %convert_bitcast_fusion = bf16[16,512,2,64]{1,3,2,0:T(8,128)(2,1)S(1)} fusion(f32[16,2,512,512]{2,3,1,0:T(8,128)} %get-tuple-element.34, f32[16,2,512]{2,1,0:T(2,128)S(1)} %get-tuple-element.33, bf16[16,512,2,3,64]{4,1,3,2,0:T(8,128)(2,1)} %bitcast.59), kind=kOutput, calls=%fused_computation.34 | convolution fusion | flops 1091567616 | bytes 39911424 | tf_op jit(solution)/shard_map/while/body/eval_jaxpr/bhqk,bkhe->bqhe/dot_general | solution.py:58
  424.2 0.0 copy-start.11
  424.2 7.7 %copy.40 = bf16[16,512,2,64]{3,2,0,1:T(2,128)(2,1)} copy(bf16[16,512,2,64]{1,3,2,0:T(8,128)(2,1)S(1)} %convert_bitcast_fusion) | data formatting | bytes 4194304 | tf_op jit(solution)/shard_map/while/body/eval_jaxpr/convert_element_type | solution.py:58
  431.9 7.5 %reshape.113 = bf16[16,2,32768]{2,1,0:T(2,128)(2,1)} reshape(bf16[512,16,2,64]{3,2,1,0:T(2,128)(2,1)} %bitcast.66) | data formatting | bytes 4194304
  439.4 8.9 %all-to-all-start.1 = ((bf16[16,2,32768]{2,1,0:T(2,128)(2,1)}), bf16[16,2,32768]{2,1,0:T(2,128)(2,1)S(1)}, u32[]{:S(2)}, u32[]{:S(2)}) async-start(bf16[16,2,32768]{2,1,0:T(2,128)(2,1)} %reshape.113), calls=%async_computation.1 | async-start | bytes 4194304 | tf_op jit(solution)/shard_map/all_to_all | solution.py:79
  448.4 5.9 %fusion.29 = (bf16[16,512,2,1,64]{4,1,3,2,0:T(8,128)(2,1)}, bf16[16,512,2,1,64]{4,1,3,2,0:T(8,128)(2,1)}) fusion(bf16[16,512,2,3,64]{4,1,3,2,0:T(8,128)(2,1)} %bitcast.60), kind=kLoop, calls=%fused_computation.47 | loop fusion | bytes 8388608 | tf_op jit(solution)/shard_map/slice | solution.py:77
  454.3 4.8 copy.47
  459.1 4.8 copy.49
  463.8 33.3 %all-to-all-done.1 = bf16[16,2,32768]{2,1,0:T(2,128)(2,1)S(1)} async-done(((bf16[16,2,32768]{2,1,0:T(2,128)(2,1)}), bf16[16,2,32768]{2,1,0:T(2,128)(2,1)S(1)}, u32[]{:S(2)}, u32[]{:S(2)}) %all-to-all-start.1) | async-done | bytes 2097184 | tf_op jit(solution)/shard_map/all_to_all | solution.py:79
  497.2 5.0 reshape.114
  502.2 0.0 copy-start.8
  502.2 4.0 copy.41
  506.1 1.3 copy.42
  507.5 9.7 %fusion.20 = bf16[16,32,2048]{2,1,0:T(8,128)(2,1)} fusion(bf16[16,32,32,64]{3,1,2,0:T(8,128)(2,1)S(1)} %bitcast.69, bf16[32,64,2048,1]{2,1,0,3:T(8,128)(2,1)} %bitcast.74, f32[2048]{0:T(1024)S(1)} %convert_element_type.70, f32[2048]{0:T(1024)S(1)} %copy-done.6, f32[2048]{0:T(1024)S(1)} %copy-done.4, f32[16,32]{1,0:T(8,128)S(1)} %copy-done.8, ...), kind=kOutput, calls=%fused_computation.32 | convolution fusion | flops 4306501632 | bytes 14708736 | tf_op jit(solution)/shard_map/bshe,hef->bsf/dot_general | solution.py:81
  (26 shorter events, 0.1 us)
Async XLA Ops:
  2.6 4.5 copy-start.1
  4.9 2.2 copy-start.7
  5.6 1.5 copy-start.3
  6.3 0.8 copy-start.5
  55.5 24.1 %copy-start.9 = (s32[16,32]{1,0:T(8,128)S(1)}, s32[16,32]{1,0:T(8,128)}, u32[]{:S(2)}) copy-start(s32[16,32]{1,0:T(8,128)} %param.12) | copy-start | bytes 6148
  55.5 24.1 %copy-start.10 = (s32[16,32]{1,0:T(8,128)S(1)}, s32[16,32]{1,0:T(8,128)}, u32[]{:S(2)}) copy-start(s32[16,32]{1,0:T(8,128)} %param.11) | copy-start | bytes 6148
  89.1 23.4 %slice-start = ((s8[8388608]{0:T(1024)(128)(4,1)}), s8[4194304]{0:T(1024)(128)(4,1)S(1)}, s32[]{:S(2)}) async-start(s8[8388608]{0:T(1024)(128)(4,1)} %bitcast.64), calls=%async_computation.2 | async-start | bytes 8388608
  97.1 15.5 %slice-start.1 = ((s8[8388608]{0:T(1024)(128)(4,1)}), s8[4194304]{0:T(1024)(128)(4,1)S(1)}, s32[]{:S(2)}) async-start(s8[8388608]{0:T(1024)(128)(4,1)} %bitcast.64), calls=%async_computation.3 | async-start | bytes 8388608
  174.6 11.0 %copy-start.12 = (s32[16]{0:T(128)S(1)}, s32[16]{0:T(128)}, u32[]{:S(2)}) copy-start(s32[16]{0:T(128)} %param.13) | copy-start | bytes 196
  174.6 152.1 %all-to-all-start = ((bf16[16,2,98304]{2,1,0:T(2,128)(2,1)}), bf16[16,2,98304]{2,1,0:T(2,128)(2,1)}, u32[]{:S(2)}, u32[]{:S(2)}) async-start(bf16[16,2,98304]{2,1,0:T(2,128)(2,1)} %reshape.111), calls=%async_computation | async-start | bytes 12582912 | tf_op jit(solution)/shard_map/all_to_all | solution.py:75
  424.2 24.1 %copy-start.11 = (bf16[2048]{0:T(1024)(128)(2,1)S(1)}, bf16[2048]{0:T(1024)(128)(2,1)}, u32[]{:S(2)}) copy-start(bf16[2048]{0:T(1024)(128)(2,1)} %param.19) | copy-start | bytes 12292
  439.4 57.7 %all-to-all-start.1 = ((bf16[16,2,32768]{2,1,0:T(2,128)(2,1)}), bf16[16,2,32768]{2,1,0:T(2,128)(2,1)S(1)}, u32[]{:S(2)}, u32[]{:S(2)}) async-start(bf16[16,2,32768]{2,1,0:T(2,128)(2,1)} %reshape.113), calls=%async_computation.1 | async-start | bytes 4194304 | tf_op jit(solution)/shard_map/all_to_all | solution.py:79
  502.1 5.3 %copy-start = (bf16[16,32,2048]{2,1,0:T(8,128)(2,1)S(1)}, bf16[16,32,2048]{2,1,0:T(8,128)(2,1)}, u32[]{:S(2)}) copy-start(bf16[16,32,2048]{2,1,0:T(8,128)(2,1)} %param.10) | copy-start | bytes 6291460
  502.1 5.3 %copy-start.2 = (f32[16,32]{1,0:T(8,128)S(1)}, f32[16,32]{1,0:T(8,128)}, u32[]{:S(2)}) copy-start(f32[16,32]{1,0:T(8,128)} %copy-done.1) | copy-start | bytes 6148
  502.1 5.3 %copy-start.4 = (f32[2048]{0:T(1024)S(1)}, f32[2048]{0:T(1024)}, u32[]{:S(2)}) copy-start(f32[2048]{0:T(1024)} %copy-done.3) | copy-start | bytes 24580
  502.1 5.3 %copy-start.6 = (f32[2048]{0:T(1024)S(1)}, f32[2048]{0:T(1024)}, u32[]{:S(2)}) copy-start(f32[2048]{0:T(1024)} %copy-done.5) | copy-start | bytes 24580
  502.2 5.3 %copy-start.8 = (f32[16,32]{1,0:T(8,128)S(1)}, f32[16,32]{1,0:T(8,128)}, u32[]{:S(2)}) copy-start(f32[16,32]{1,0:T(8,128)} %copy-done.7) | copy-start | bytes 6148
where the time goes:
time: 520 us; the launch traced here: 517 us
  waiting for transfers between devices  171 us (33%)
  local copies, waits for them, and re-layouts  155 us (30%)
  other arithmetic  97.1 us (19%)
  matrix products  74 us (14%)
  starting transfers between devices  19.8 us (4%)
    all_to_all x1, waiting for transfers between devices, local_block(): by_heads = lax.all_to_all(qkv_rot, 'sp', 2, 1, tiled=True)  137 us
    unnamed x36, local copies, waits for them, and re-layouts  55.1 us
    sub x1, other arithmetic, attend_block(): jax.nn.softmax(jnp.where(visible, scores, -jnp.inf), axis=-1)  37.1 us
    all_to_all x1, waiting for transfers between devices, local_block(): by_tokens = lax.all_to_all(context, 'sp', 1, 2, tiled=True)  33.3 us
    dot_general x1, matrix products, local_block(): jnp.einsum('bsd,dhte->bshte', normed, w_qkv, preferred_element_type=jnp.f...  31.7 us
    concatenate x1, local copies, waits for them, and re-layouts, local_block(): qkv_rot = jnp.concatenate([qk_rot, qkv_proj[:, :, :, 2:]], axis=3)  29.6 us
    reshape x1, local copies, waits for them, and re-layouts, rotate_pairs(): qk_pair.astype(jnp.float32)  24 us
    dot_general x1, matrix products, attend_block(): jnp.einsum('bqhe,bkhe->bhqk', q_block, key_heads, preferred_element_type=...  19.1 us
  transfers between devices with their start and end apart: 2, of which 2 were waited for; matrix products, arithmetic and copies ran while one was open for 4% of the time, Pallas kernels for 0%

commit v1 on v0

v1 whole, which is shorter than its diff:
```python
import functools
import math

import jax
import jax.numpy as jnp
from jax import lax
from jax.experimental import pallas as pl
from jax.experimental.pallas import tpu as pltpu
from jax.sharding import PartitionSpec as P

ALPHA = math.sqrt(56.0)
ROPE_BASE = 10000.0
LN_EPS = 1e-5
CORES = 2
CHUNKS = 4
LANES = 128
QUERY_TILE = 128
CTX_MIN = 128
CTX_MAX = 384
LN_ROWS = 32
DENSE_COLS = 512
MESH = pl.DeviceIdType.MESH
NT = (((1,), (1,)), ((), ()))


def ring_order(n):
    order = []
    for step in range(1, n // 2):
        order += [step, n - step]
    return order + [n // 2]


def block_kernel(n, rows, toks, dh, hidden, w_hbm, b_qkv, wd_hbm, vecs, ctx, last_pos, freq,
                 out, k_out, v_out,
                 w_v, wd_v, a_v, fwd, qkv, cs, cr, ob, kvs, m_v,
                 h_sem, w_sem, wd_sem, a_send, a_recv, f_send, q_recv, c_send, c_recv, m_send, m_recv, kv_sem, o_sem):
    me = lax.axis_index('sp')
    chips = n // CORES
    chip, core = me // CORES, me % CORES
    part = rows // CHUNKS
    chunk = part * toks
    width = a_v.shape[2]
    seq = n * toks
    hl = w_hbm.shape[1]

    def device(chip_index, core_index):
        return {'sp': (chip_index % chips) * CORES + core_index}

    hidden_copies = []
    for k in range(CHUNKS):
        copy = pltpu.make_async_copy(hidden.at[pl.ds(k * chunk, chunk)], a_v.at[0, pl.ds(k * chunk, chunk)], h_sem.at[k])
        copy.start()
        hidden_copies.append(copy)

    def weight_copy(slot, block):
        for h in range(hl):
            for t in range(3):
                pltpu.make_async_copy(w_hbm.at[block, h, t], w_v.at[slot, t, h], w_sem.at[slot]).start()

    weight_blocks = [(0, 0), (0, 1), (1, 0), (1, 1), (2, 0), (2, 1), (-1, 0), (-1, 1), (-2, 0), (-2, 1), (3, 0), (-3, 1)]
    for slot, (step, kore) in enumerate(weight_blocks):
        weight_copy(slot, ((chip + step + chips) % chips) * CORES + kore)
    wd_copy = pltpu.make_async_copy(wd_hbm, wd_v, wd_sem)
    wd_copy.start()

    barrier = pltpu.get_barrier_semaphore()
    for step in range(1, n):
        pl.semaphore_signal(barrier, inc=1, device_id={'sp': (me + step) % n}, device_id_type=MESH)
    pl.semaphore_wait(barrier, n - 1)

    @pl.when(me == n - 1)
    def _():
        for step in range(1, n):
            pltpu.make_async_remote_copy(src_ref=last_pos, dst_ref=m_v, send_sem=m_send.at[step], recv_sem=m_recv,
                                         device_id={'sp': (me + step) % n}, device_id_type=MESH).start()

    def a_copy(k, side):
        peer = device(chip + 1 - 2 * side + chips, core)
        return pltpu.make_async_remote_copy(src_ref=a_v.at[0, pl.ds(k * chunk, chunk)],
                                            dst_ref=a_v.at[1 + side, pl.ds(k * chunk, chunk)],
                                            send_sem=a_send.at[side, k], recv_sem=a_recv.at[side, k],
                                            device_id=peer, device_id_type=MESH)

    gamma = vecs[0:1, :]
    beta = vecs[1:2, :]
    for k in range(CHUNKS):
        hidden_copies[k].wait()

        def norm_rows(i, carry):
            at = pl.ds(pl.multiple_of(k * chunk + i * LN_ROWS, LN_ROWS), LN_ROWS)
            x = a_v[0, at, :].astype(jnp.float32)
            mean = jnp.mean(x, axis=-1, keepdims=True)
            centered = x - mean
            var = jnp.mean(jnp.square(centered), axis=-1, keepdims=True)
            a_v[0, at, :] = (centered * lax.rsqrt(var + LN_EPS) * gamma + beta).astype(jnp.bfloat16)
            return carry

        lax.fori_loop(0, chunk // LN_ROWS, norm_rows, 0)
        for side in range(2):
            a_copy(k, side).start()

    def project(source, k, slot, count, block):
        a = a_v[source, pl.ds(pl.multiple_of(k * chunk, chunk), chunk), :]
        w = w_v[pl.ds(slot, count)].reshape(count * 3 * hl * dh, width)
        acc = lax.dot_general(a, w, NT, preferred_element_type=jnp.float32)
        cols = 3 * hl * dh
        return [(acc[:, i * cols:(i + 1) * cols] + b_qkv[block + i]).astype(jnp.bfloat16).reshape(part, toks, cols) for i in range(count)]

    def owner_at(k, owner):
        return pl.ds(k * part, part), pl.ds(pl.multiple_of(owner * toks, toks), toks)

    def send(value, k, slot, owner, dest):
        fwd[slot, k] = value
        at = owner_at(k, owner)
        pltpu.make_async_remote_copy(src_ref=fwd.at[slot, k], dst_ref=qkv.at[at[0], at[1]], send_sem=f_send, recv_sem=q_recv.at[k],
                                     device_id=dest, device_id_type=MESH).start()

    def to_own_chip(source, k, owner):
        values = project(source, k, 0, CORES, chip * CORES)
        for h in range(CORES):
            @pl.when(core == h)
            def _():
                at = owner_at(k, owner)
                qkv[at[0], at[1], :] = values[h]
                send(values[CORES - 1 - h], k, source, owner, device(chip, CORES - 1 - h))

    def wait_weights(slot):
        pltpu.make_async_copy(w_v.at[slot], w_v.at[slot], w_sem.at[slot]).wait()

    for slot in range(CORES):
        wait_weights(slot)

    def own_chunk(k, carry):
        to_own_chip(0, k, me)
        return carry

    lax.fori_loop(0, CHUNKS, own_chunk, 0)
    for slot in range(CORES, len(weight_blocks)):
        wait_weights(slot)

    def neighbour(side):
        return ((chip - 1 + 2 * side + chips) % chips) * CORES + core

    def forward_chunk(k, carry):
        for side in range(2):
            a_copy(k, side).wait_recv()

        def pair(index, c):
            side, step = index // 2, index % 2 + 1
            owner = neighbour(side)
            target = (chip + (1 - 2 * side) * step + chips) % chips
            values = project(1 + side, k, CORES + CORES * index, CORES, target * CORES)
            for h in range(CORES):
                send(values[h], k, 3 + CORES * index + h, owner, device(target, h))
            return c

        def single(side, c):
            owner = neighbour(side)
            target = (chip + (1 - 2 * side) * 3 + chips) % chips
            values = project(1 + side, k, 10 + side, 1, target * CORES + side)
            send(values[0], k, 11 + side, owner, device(target, side))
            return c

        def own(side, c):
            to_own_chip(1 + side, k, neighbour(side))
            return c

        lax.fori_loop(0, 4, pair, 0)
        lax.fori_loop(0, 2, single, 0)
        lax.fori_loop(0, 2, own, 0)
        return carry

    lax.fori_loop(0, CHUNKS, forward_chunk, 0)

    @pl.when(me == n - 1)
    def _():
        m_v[...] = last_pos[...]

    @pl.when(me != n - 1)
    def _():
        pltpu.make_async_copy(last_pos, m_v, m_recv).wait()

    row_iota = lax.broadcasted_iota(jnp.int32, (seq, LANES), 0)
    lane = lax.broadcasted_iota(jnp.int32, (seq, LANES), 1)
    pair_low = lane % (dh // 2) < dh // 4
    by_pos = lane % dh < dh // 2
    n_tiles = seq // QUERY_TILE

    def attend_row(b):
        ctx_b = ctx[pl.ds(b, 1), :]
        in_ctx = row_iota < ctx_b
        pos = jnp.where(in_ctx, row_iota.astype(jnp.float32), m_v[pl.ds(b, 1), :])
        blk = jnp.where(in_ctx, 0, row_iota - ctx_b + 1).astype(jnp.float32)
        angle = jnp.where(by_pos, pos, blk) * freq[...]
        cos = jnp.cos(angle)
        sin = jnp.sin(angle)
        sin = jnp.where(pair_low, -sin, sin)

        def rotate(x):
            swapped = jnp.where(pair_low, pltpu.roll(x, LANES - dh // 4, 1), pltpu.roll(x, dh // 4, 1))
            return x * cos + swapped * sin

        q = rotate(qkv[b, :, 0:LANES].astype(jnp.float32)) * (1.0 / math.sqrt(dh))
        k = rotate(qkv[b, :, LANES:2 * LANES].astype(jnp.float32))
        v_raw = qkv[b, :, 2 * LANES:3 * LANES]
        v = v_raw.astype(jnp.float32)
        slot = b % 2

        @pl.when(b >= 2)
        def _():
            pltpu.make_async_copy(kvs.at[slot], kvs.at[slot], kv_sem.at[slot]).wait()

        kvs[slot, 0] = k.astype(jnp.bfloat16).T
        kvs[slot, 1] = v_raw.T
        pltpu.make_async_copy(kvs.at[slot, 0], k_out.at[b], kv_sem.at[slot]).start()
        pltpu.make_async_copy(kvs.at[slot, 1], v_out.at[b], kv_sem.at[slot]).start()

        heads = []
        for h in range(hl):
            mine = lane // dh == h
            heads.append([jnp.where(mine, x, 0.0).astype(jnp.bfloat16) for x in (q, k, v)])
        for qt in range(n_tiles):
            start = qt * QUERY_TILE
            rows_here = slice(start, start + QUERY_TILE)
            keys_here = max(CTX_MAX, start + QUERY_TILE)
            bound = jnp.maximum(ctx_b, row_iota[rows_here] + 1)
            total = None
            for q_h, k_h, v_h in heads:
                s = lax.dot_general(q_h[rows_here], k_h[:keys_here], NT, preferred_element_type=jnp.float32)
                tiles = []
                for kt in range(keys_here // LANES):
                    tile = s[:, kt * LANES:(kt + 1) * LANES]
                    last_key = (kt + 1) * LANES - 1
                    if last_key >= CTX_MIN and last_key > start:
                        tile = jnp.where(lane[rows_here] + kt * LANES < bound, tile, -jnp.inf)
                    tiles.append(tile)
                top = functools.reduce(jnp.maximum, tiles)
                top = jnp.max(top, axis=-1, keepdims=True)
                tiles = [jnp.exp(tile - top) for tile in tiles]
                norm = jnp.sum(functools.reduce(jnp.add, tiles), axis=-1, keepdims=True)
                inv = 1.0 / norm
                probs = jnp.concatenate([(tile * inv).astype(jnp.bfloat16) for tile in tiles], axis=1)
                o = jnp.dot(probs, v_h[:keys_here], preferred_element_type=jnp.float32)
                total = o if total is None else total + o
            owners = QUERY_TILE // toks
            cs[pl.ds(qt * owners, owners), b] = total.astype(jnp.bfloat16).reshape(owners, toks, LANES)

    def attend_chunk(kk, carry):
        some = qkv.at[pl.ds(kk * part, part), pl.ds(0, 13 * toks)]
        pltpu.make_async_copy(some, some, q_recv.at[kk]).wait()

        def one_row(r, c):
            attend_row(kk * part + r)
            return c

        lax.fori_loop(0, part, one_row, 0)
        rows_k = pl.ds(kk * part, part)
        cols_me = pl.ds(pl.multiple_of(me * LANES, LANES), LANES)
        for step in ring_order(n):
            dest = (me + step) % n
            pltpu.make_async_remote_copy(src_ref=cs.at[dest, rows_k], dst_ref=cr.at[rows_k, :, cols_me], send_sem=c_send,
                                         recv_sem=c_recv.at[kk], device_id={'sp': dest}, device_id_type=MESH).start()
        cr[rows_k, :, cols_me] = cs[me, rows_k]
        return carry

    lax.fori_loop(0, CHUNKS, attend_chunk, 0)
    wd_copy.wait()

    def out_copy(kk, slot):
        return pltpu.make_async_copy(ob.at[slot], out.at[pl.ds(pl.multiple_of(kk * chunk, chunk), chunk)], o_sem.at[slot])

    def dense_chunk(kk, carry):
        some = cr.at[pl.ds(kk * part, part), :, pl.ds(0, (n - 1) * LANES)]
        pltpu.make_async_copy(some, some, c_recv.at[kk]).wait()
        slot = kk % 2

        @pl.when(kk >= 2)
        def _():
            out_copy(kk - 2, slot).wait()

        def columns(j, c):
            at = pl.ds(pl.multiple_of(j * DENSE_COLS, DENSE_COLS), DENSE_COLS)
            x = cr[pl.ds(kk * part, part)].reshape(chunk, width)
            dense = jnp.dot(x, wd_v[:, at], preferred_element_type=jnp.float32) + vecs[2:3, at]
            a = a_v[0, pl.ds(pl.multiple_of(kk * chunk, chunk), chunk), at].astype(jnp.float32)
            ob[slot, :, at] = (a * ALPHA + dense).astype(jnp.bfloat16)
            return c

        lax.fori_loop(0, width // DENSE_COLS, columns, 0)
        out_copy(kk, slot).start()
        return carry

    lax.fori_loop(0, CHUNKS, dense_chunk, 0)

    for kk in range(CHUNKS - 2, CHUNKS):
        out_copy(kk, kk % 2).wait()
    for slot in range(2):
        pltpu.make_async_copy(kvs.at[slot], kvs.at[slot], kv_sem.at[slot]).wait()
    for k in range(CHUNKS):
        for side in range(2):
            a_copy(k, side).wait_send()
    pltpu.make_async_copy(fwd, fwd, f_send).wait()
    sent = cs.at[pl.ds(0, n - 1)]
    pltpu.make_async_copy(sent, sent, c_send).wait()

    @pl.when(me == n - 1)
    def _():
        for step in range(1, n):
            pltpu.make_async_copy(last_pos, m_v, m_send.at[step]).wait()


def solution(mesh):
    n = mesh.shape['sp']
    seq_spec = P('dp', 'sp', None)
    row_spec = P('dp', 'sp')
    head_spec = P('dp', None, 'sp', None)
    replicated = P()

    def local_block(hidden, pos_ids, block_ids, ctx_len, ln_gamma, ln_beta, w_qkv, b_qkv, w_dense, b_dense):
        rows, toks, width = hidden.shape
        heads, _, dh = b_qkv.shape
        hl = heads // n
        seq = n * toks
        tokens = rows * toks
        part = rows // CHUNKS
        cols = 3 * hl * dh
        w_t = jnp.transpose(w_qkv, (1, 2, 3, 0)).reshape(n, hl, 3, dh, width)
        bias = jnp.transpose(b_qkv.astype(jnp.float32).reshape(n, hl, 3, dh), (0, 2, 1, 3)).reshape(n, 1, cols)
        vecs = jnp.stack([ln_gamma, ln_beta, b_dense]).astype(jnp.float32)
        ctx = jnp.broadcast_to(ctx_len[:, None], (rows, LANES))
        last_pos = jnp.broadcast_to(pos_ids[:, -1:].astype(jnp.float32), (rows, LANES))
        half = dh // 2
        inv_freq = ROPE_BASE ** (-jnp.arange(0, half, 2).astype(jnp.float32) / half)
        freq = jnp.tile(inv_freq, LANES // inv_freq.shape[0])[None, :]
        vmem = pl.BlockSpec(memory_space=pltpu.VMEM)
        anywhere = pl.BlockSpec(memory_space=pl.ANY)
        out, k_out, v_out = pl.pallas_call(
            functools.partial(block_kernel, n, rows, toks, dh),
            out_shape=[jax.ShapeDtypeStruct((tokens, width), jnp.bfloat16)] + [jax.ShapeDtypeStruct((rows, hl * dh, seq), jnp.bfloat16)] * 2,
            in_specs=[anywhere, anywhere, vmem, anywhere, vmem, vmem, vmem, vmem],
            out_specs=[anywhere] * 3,
            scratch_shapes=[
                pltpu.VMEM((12, 3, hl, dh, width), jnp.bfloat16),
                pltpu.VMEM((width, width), jnp.bfloat16),
                pltpu.VMEM((3, tokens, width), jnp.bfloat16),
                pltpu.VMEM((13, CHUNKS, part, toks, cols), jnp.bfloat16),
                pltpu.VMEM((rows, seq, cols), jnp.bfloat16),
                pltpu.VMEM((n, rows, toks, LANES), jnp.bfloat16),
                pltpu.VMEM((rows, toks, width), jnp.bfloat16),
                pltpu.VMEM((2, part * toks, width), jnp.bfloat16),
                pltpu.VMEM((2, 2, hl * dh, seq), jnp.bfloat16),
                pltpu.VMEM((rows, LANES), jnp.float32),
                pltpu.SemaphoreType.DMA((CHUNKS,)),
                pltpu.SemaphoreType.DMA((12,)),
                pltpu.SemaphoreType.DMA,
                pltpu.SemaphoreType.DMA((2, CHUNKS)),
                pltpu.SemaphoreType.DMA((2, CHUNKS)),
                pltpu.SemaphoreType.DMA,
                pltpu.SemaphoreType.DMA((CHUNKS,)),
                pltpu.SemaphoreType.DMA,
                pltpu.SemaphoreType.DMA((CHUNKS,)),
                pltpu.SemaphoreType.DMA((n,)),
                pltpu.SemaphoreType.DMA,
                pltpu.SemaphoreType.DMA((2,)),
                pltpu.SemaphoreType.DMA((2,)),
            ],
            compiler_params=pltpu.CompilerParams(collective_id=0, has_side_effects=True, vmem_limit_bytes=66_000_000),
            name='attention_block',
        )(hidden.reshape(tokens, width), w_t, bias, w_dense, vecs, ctx, last_pos, freq)

        def to_heads(x):
            return jnp.transpose(x.reshape(rows, hl, dh, seq), (0, 3, 1, 2))

        return out.reshape(rows, toks, width), to_heads(k_out), to_heads(v_out)

    return jax.shard_map(local_block, mesh=mesh, in_specs=(seq_spec, row_spec, row_spec, P('dp'), replicated, replicated, replicated, replicated, replicated, replicated), out_specs=(seq_spec, head_spec, head_spec), check_vma=False)
```

time: 520 us -> 203 us (0.39)
  Pallas kernels: 0 us -> 187 us
  waiting for transfers between devices: 171 us -> 0 us
  local copies, waits for them, and re-layouts: 155 us -> 12.4 us
  other arithmetic: 97.1 us -> 2.29 us
  matrix products: 74 us -> 0 us
  starting transfers between devices: 19.8 us -> 0 us
    pallas_call x0 -> x1, Pallas kernels: none -> 187 us  [local_block(): pl.pallas_call(functools.partial(block_kernel, n, rows, toks, dh), out_sh...]
    all_to_all x2 -> x0, waiting for transfers between devices: 171 us -> none  [the longest x1 137 us: local_block(): by_heads = lax.all_to_all(qkv_rot, 'sp', 2, 1, tiled=True)]
    dot_general x4 -> x0, matrix products: 74 us -> none  [the longest x1 31.7 us: local_block(): jnp.einsum('bsd,dhte->bshte', normed, w_qkv, preferred_element_type=jnp.f...]
    unnamed x36 -> x7, local copies, waits for them, and re-layouts: 55.1 us -> 6.98 us
    sub x1 -> x0, other arithmetic: 37.1 us -> none  [attend_block(): jax.nn.softmax(jnp.where(visible, scores, -jnp.inf), axis=-1)]
    concatenate x1 -> x0, local copies, waits for them, and re-layouts: 29.6 us -> none  [local_block(): qkv_rot = jnp.concatenate([qk_rot, qkv_proj[:, :, :, 2:]], axis=3)]
    reshape x1, local copies, waits for them, and re-layouts: 24 us -> 0.71 us  [local_block(): jnp.transpose(b_qkv.astype(jnp.float32).reshape(n, hl, 3, dh), (0, 2, 1, 3))]
    slice x3 -> x0, local copies, waits for them, and re-layouts: 20.6 us -> none  [the longest x2 14.6 us: local_block(): qkv_rot = jnp.concatenate([qk_rot, qkv_proj[:, :, :, 2:]], axis=3)]
  transfers between devices with their start and end apart: 2 -> 0, of which waited for: 2 -> 0; matrix products, arithmetic and copies ran while one was open for 4% -> 0% of each run, Pallas kernels for 0% -> 0%
where the time goes in v1:
time: 203 us
  Pallas kernels  187 us (92%)
  local copies, waits for them, and re-layouts  12.4 us (6%)
  other arithmetic  2.29 us (1%)
    pallas_call x1, Pallas kernels, local_block(): pl.pallas_call(functools.partial(block_kernel, n, rows, toks, dh), out_sh...  187 us
    unnamed x7, local copies, waits for them, and re-layouts  6.98 us

profile of v1, /device:TPU:21, one launch (start us, length us, event | category | flops | bytes accessed | tf_op | source)
XLA Modules:
  0.0 202.7 jit_solution(2869827596043696338)
XLA Ops:
  0.6 0.9 convert_reduce_fusion
  1.5 0.7 broadcast_in_dim_tile.3.freq
  2.2 0.7 broadcast_in_dim.15.last_pos
  2.8 1.3 broadcast_in_dim.6.ctx
  4.2 0.7 stack.12
  4.9 0.7 stack.13
  5.6 0.7 stack.14
  6.3 0.6 maximum_convert_fusion.vecs
  6.9 0.8 copy_bitcast_fusion
  7.7 0.7 reshape.48.b_qkv
  8.4 187.3 %attention_block.1 = (bf16[512,2048]{1,0:T(8,128)(2,1)}, bf16[16,128,512]{2,1,0:T(8,128)(2,1)}, bf16[16,128,512]{2,1,0:T(8,128)(2,1)}) custom-call(bf16[512,2048]{1,0:T(8,128)(2,1)} %bitcast.21, bf16[16,2,3,64,2048]{4,3,2,1,0:T(8,128)(2,1)} %bitcast.17, f32[16,1,384]{2,1,0:T(1,128)} %reshape.48.b_qkv, bf16[2048,2048]{1,0:T(8,128)(2,1)} %wd_hbm.1, ...), custom_call_target="tpu_custom_call" | custom-call | tf_op jit(solution)/shard_map/attention_block/pallas_call | solution.py:337
  195.7 0.0 copy-start.1
  195.7 3.3 %copy.18 = bf16[16,32,2048]{2,1,0:T(8,128)(2,1)} copy(bf16[16,32,2048]{2,1,0:T(8,128)(2,1)} %bitcast.20) | data formatting | bytes 4194304
  199.0 0.0 copy-done.1
  199.0 0.0 copy-start
  199.0 1.3 copy.19
  200.3 1.0 copy-done
  201.4 1.3 copy.20
  (2 shorter events, 0.0 us)
Async XLA Ops:
  195.7 3.3 %copy-start.1 = (bf16[16,128,512]{2,1,0:T(8,128)(2,1)S(1)}, bf16[16,128,512]{2,1,0:T(8,128)(2,1)}, u32[]{:S(2)}) copy-start(bf16[16,128,512]{2,1,0:T(8,128)(2,1)} %get-tuple-element.7) | copy-start | bytes 6291460
  199.0 2.3 %copy-start = (bf16[16,128,512]{2,1,0:T(8,128)(2,1)S(1)}, bf16[16,128,512]{2,1,0:T(8,128)(2,1)}, u32[]{:S(2)}) copy-start(bf16[16,128,512]{2,1,0:T(8,128)(2,1)} %get-tuple-element.8) | copy-start | bytes 6291460

commit v2 on v1

v2 whole, which is shorter than its diff:
```python
import functools
import math

import jax
import jax.numpy as jnp
import numpy as np
from jax import lax
from jax.experimental import pallas as pl
from jax.experimental.pallas import tpu as pltpu
from jax.sharding import PartitionSpec as P

ALPHA = math.sqrt(56.0)
ROPE_BASE = 10000.0
LN_EPS = 1e-5
CORES = 2
CHUNKS = 4
LANES = 128
QUERY_TILE = 128
CTX_MIN = 128
CTX_MAX = 384
FIRST_ROWS = 4
DENSE_COLS = 512
MESH = pl.DeviceIdType.MESH
NT = (((1,), (1,)), ((), ()))


def far_first(n):
    half = n // 2
    order = [half]
    for step in range(1, half):
        order += [half - step, half + step]
    return order


def block_kernel(n, rows, toks, dh, hidden, w_hbm, bq_hbm, wd_hbm, gamma_hbm, beta_hbm, bd_hbm, ctx_hbm, pos_hbm, freq_hbm,
                 out_v, k_v, v_v, wd_v, last_v, rest_v,
                 w_v, a_v, fwd, qkv, cs, cr, bq_v, bias, g_v, be_v, bd_v, vecs, ctx, pos_v, m_v, freq,
                 h_sem, w_sem, wd_sem, small_sem, a_send, a_recv, f_send, q_recv, c_send, c_recv, m_send, m_recv):
    me = lax.axis_index('sp')
    chips = n // CORES
    chip, core = me // CORES, me % CORES
    part = rows // CHUNKS
    chunk = part * toks
    width = a_v.shape[2]
    seq = n * toks
    hl = w_hbm.shape[1]

    def device(chip_index, core_index):
        return {'sp': (chip_index % chips) * CORES + core_index}

    barrier = pltpu.get_barrier_semaphore()
    for step in range(1, n):
        pl.semaphore_signal(barrier, inc=1, device_id={'sp': (me + step) % n}, device_id_type=MESH)

    def row_at(r):
        return pl.ds(pl.multiple_of(r * toks, toks), toks)

    def hidden_copy(r):
        return pltpu.make_async_copy(hidden.at[row_at(r)], a_v.at[0, row_at(r)], h_sem.at[r])

    small = [(gamma_hbm, g_v), (beta_hbm, be_v), (bd_hbm, bd_v), (bq_hbm, bq_v), (ctx_hbm, ctx), (pos_hbm, pos_v), (freq_hbm, freq)]
    small_copies = [pltpu.make_async_copy(src, dst, small_sem.at[i]) for i, (src, dst) in enumerate(small)]
    for copy in small_copies[:2]:
        copy.start()
    for r in range(rows):
        hidden_copy(r).start()
    for copy in small_copies[2:]:
        copy.start()
    for i in range(2):
        small_copies[i].wait()
        vecs[i:i + 1, :] = small[i][1][...].astype(jnp.float32)[None, :]
    pl.semaphore_wait(barrier, n - 1)

    def a_copy(start, size, k, side):
        peer = device(chip + 1 - 2 * side + chips, core)
        at = pl.ds(start, size)
        return pltpu.make_async_remote_copy(src_ref=a_v.at[0, at], dst_ref=a_v.at[1 + side, at],
                                            send_sem=a_send.at[side], recv_sem=a_recv.at[side, k],
                                            device_id=peer, device_id_type=MESH)

    def norm_row(r, carry):
        hidden_copy(r).wait()
        x = a_v[0, row_at(r), :].astype(jnp.float32)
        mean = jnp.mean(x, axis=-1, keepdims=True)
        centered = x - mean
        var = jnp.mean(jnp.square(centered), axis=-1, keepdims=True)
        a_v[0, row_at(r), :] = (centered * lax.rsqrt(var + LN_EPS) * vecs[0:1, :] + vecs[1:2, :]).astype(jnp.bfloat16)
        for side in range(2):
            a_copy(pl.multiple_of(r * toks, toks), toks, r // part, side).start()
        return carry

    lax.fori_loop(0, FIRST_ROWS, norm_row, 0)

    def weight_copy(slot, block):
        for h in range(hl):
            for t in range(3):
                pltpu.make_async_copy(w_hbm.at[block, h, t], w_v.at[slot, t, h], w_sem.at[slot]).start()

    weight_blocks = [(0, 0), (0, 1), (1, 0), (1, 1), (2, 0), (2, 1), (-1, 0), (-1, 1), (-2, 0), (-2, 1), (3, 0), (-3, 1)]
    for slot, (step, kore) in enumerate(weight_blocks):
        weight_copy(slot, ((chip + step + chips) % chips) * CORES + kore)
    wd_copy = pltpu.make_async_copy(wd_hbm, wd_v, wd_sem)
    wd_copy.start()
    lax.fori_loop(FIRST_ROWS, rows, norm_row, 0)

    for copy in small_copies[2:]:
        copy.wait()
    vecs[2:3, :] = bd_v[...].astype(jnp.float32)[None, :]
    raw = bq_v[...].astype(jnp.float32)
    for d in range(n):
        for t in range(3):
            bias[d, :, t * hl * dh:(t + 1) * hl * dh] = jnp.concatenate([raw[t, hl * d + h:hl * d + h + 1] for h in range(hl)], axis=1)

    @pl.when(me == n - 1)
    def _():
        for step in range(1, n):
            pltpu.make_async_remote_copy(src_ref=pos_v, dst_ref=m_v, send_sem=m_send.at[step], recv_sem=m_recv,
                                         device_id={'sp': (me + step) % n}, device_id_type=MESH).start()
        m_v[...] = pos_v[...]

    def project(source, k, slot, count, block):
        a = a_v[source, pl.ds(pl.multiple_of(k * chunk, chunk), chunk), :]
        w = w_v[pl.ds(slot, count)].reshape(count * 3 * hl * dh, width)
        acc = lax.dot_general(a, w, NT, preferred_element_type=jnp.float32)
        cols = 3 * hl * dh
        return [(acc[:, i * cols:(i + 1) * cols] + bias[block + i]).astype(jnp.bfloat16).reshape(part, toks, cols) for i in range(count)]

    def owner_at(k, owner):
        return pl.ds(k * part, part), pl.ds(pl.multiple_of(owner * toks, toks), toks)

    def send(value, k, slot, owner, dest):
        fwd[slot, k] = value
        at = owner_at(k, owner)
        pltpu.make_async_remote_copy(src_ref=fwd.at[slot, k], dst_ref=qkv.at[at[0], at[1]], send_sem=f_send, recv_sem=q_recv.at[k],
                                     device_id=dest, device_id_type=MESH).start()

    def to_own_chip(source, k, owner):
        values = project(source, k, 0, CORES, chip * CORES)
        for h in range(CORES):
            @pl.when(core == h)
            def _():
                at = owner_at(k, owner)
                qkv[at[0], at[1], :] = values[h]
                send(values[CORES - 1 - h], k, source, owner, device(chip, CORES - 1 - h))

    def wait_weights(slot):
        pltpu.make_async_copy(w_v.at[slot], w_v.at[slot], w_sem.at[slot]).wait()

    for slot in range(CORES):
        wait_weights(slot)

    def own_chunk(k, carry):
        to_own_chip(0, k, me)
        return carry

    lax.fori_loop(0, CHUNKS, own_chunk, 0)
    for slot in range(CORES, len(weight_blocks)):
        wait_weights(slot)

    def neighbour(side):
        return ((chip - 1 + 2 * side + chips) % chips) * CORES + core

    def forward_chunk(k, carry):
        for side in range(2):
            a_copy(pl.multiple_of(k * chunk, chunk), chunk, k, side).wait_recv()

        def single(side, c):
            owner = neighbour(side)
            target = (chip + (1 - 2 * side) * 3 + chips) % chips
            values = project(1 + side, k, 10 + side, 1, target * CORES + side)
            send(values[0], k, 11 + side, owner, device(target, side))
            return c

        def pair(i, c):
            side, step = i % 2, 2 - i // 2
            index = 2 * side + step - 1
            owner = neighbour(side)
            target = (chip + (1 - 2 * side) * step + chips) % chips
            values = project(1 + side, k, CORES + CORES * index, CORES, target * CORES)
            for h in range(CORES):
                send(values[h], k, 3 + CORES * index + h, owner, device(target, h))
            return c

        def own(side, c):
            to_own_chip(1 + side, k, neighbour(side))
            return c

        lax.fori_loop(0, 2, single, 0)
        lax.fori_loop(0, 4, pair, 0)
        lax.fori_loop(0, 2, own, 0)
        return carry

    lax.fori_loop(0, CHUNKS, forward_chunk, 0)

    @pl.when(me != n - 1)
    def _():
        pltpu.make_async_copy(pos_v, m_v, m_recv).wait()

    row_iota = lax.broadcasted_iota(jnp.int32, (seq, LANES), 0)
    lane = lax.broadcasted_iota(jnp.int32, (seq, LANES), 1)
    pair_low = lane % (dh // 2) < dh // 4
    by_pos = lane % dh < dh // 2
    n_tiles = seq // QUERY_TILE
    last_lane = lax.broadcasted_iota(jnp.int32, (1, toks), 1) == toks - 1

    def attend_row(b):
        ctx_b = ctx[b]
        m_b = jnp.sum(jnp.where(last_lane, m_v[pl.ds(b, 1), :].astype(jnp.float32), 0.0), axis=-1, keepdims=True)
        in_ctx = row_iota < ctx_b
        pos = jnp.where(in_ctx, row_iota.astype(jnp.float32), m_b)
        blk = jnp.where(in_ctx, 0, row_iota - ctx_b + 1).astype(jnp.float32)
        angle = jnp.where(by_pos, pos, blk) * freq[...]
        cos = jnp.cos(angle)
        sin = jnp.sin(angle)
        sin = jnp.where(pair_low, -sin, sin)

        def rotate(x):
            swapped = jnp.where(pair_low, pltpu.roll(x, LANES - dh // 4, 1), pltpu.roll(x, dh // 4, 1))
            return x * cos + swapped * sin

        q = rotate(qkv[b, :, 0:LANES].astype(jnp.float32)) * (1.0 / math.sqrt(dh))
        k = rotate(qkv[b, :, LANES:2 * LANES].astype(jnp.float32))
        v_raw = qkv[b, :, 2 * LANES:3 * LANES]
        v = v_raw.astype(jnp.float32)
        k_v[b] = k.astype(jnp.bfloat16).T
        v_v[b] = v_raw.T

        heads = []
        for h in range(hl):
            mine = lane // dh == h
            heads.append([jnp.where(mine, x, 0.0).astype(jnp.bfloat16) for x in (q, k, v)])
        for qt in range(n_tiles):
            start = qt * QUERY_TILE
            rows_here = slice(start, start + QUERY_TILE)
            keys_here = max(CTX_MAX, start + QUERY_TILE)
            bound = jnp.maximum(ctx_b, row_iota[rows_here] + 1)
            total = None
            for q_h, k_h, v_h in heads:
                s = lax.dot_general(q_h[rows_here], k_h[:keys_here], NT, preferred_element_type=jnp.float32)
                tiles = []
                for kt in range(keys_here // LANES):
                    tile = s[:, kt * LANES:(kt + 1) * LANES]
                    last_key = (kt + 1) * LANES - 1
                    if last_key >= CTX_MIN and last_key > start:
                        tile = jnp.where(lane[rows_here] + kt * LANES < bound, tile, -jnp.inf)
                    tiles.append(tile)
                top = functools.reduce(jnp.maximum, tiles)
                top = jnp.max(top, axis=-1, keepdims=True)
                tiles = [jnp.exp(tile - top) for tile in tiles]
                norm = jnp.sum(functools.reduce(jnp.add, tiles), axis=-1, keepdims=True)
                inv = 1.0 / norm
                probs = jnp.concatenate([(tile * inv).astype(jnp.bfloat16) for tile in tiles], axis=1)
                o = jnp.dot(probs, v_h[:keys_here], preferred_element_type=jnp.float32)
                total = o if total is None else total + o
            owners = QUERY_TILE // toks
            cs[pl.ds(qt * owners, owners), b] = total.astype(jnp.bfloat16).reshape(owners, toks, LANES)

    def attend_chunk(kk, carry):
        some = qkv.at[pl.ds(kk * part, part), pl.ds(0, 13 * toks)]
        pltpu.make_async_copy(some, some, q_recv.at[kk]).wait()

        def one_row(r, c):
            attend_row(kk * part + r)
            return c

        lax.fori_loop(0, part, one_row, 0)
        rows_k = pl.ds(kk * part, part)
        cols_me = pl.ds(pl.multiple_of(me * LANES, LANES), LANES)
        for step in far_first(n):
            dest = (me + step) % n
            pltpu.make_async_remote_copy(src_ref=cs.at[dest, rows_k], dst_ref=cr.at[rows_k, :, cols_me], send_sem=c_send,
                                         recv_sem=c_recv.at[kk], device_id={'sp': dest}, device_id_type=MESH).start()
        cr[rows_k, :, cols_me] = cs[me, rows_k]
        return carry

    lax.fori_loop(0, CHUNKS, attend_chunk, 0)
    wd_copy.wait()

    def context_wait(kk):
        some = cr.at[pl.ds(kk * part, part), :, pl.ds(0, (n - 1) * LANES)]
        pltpu.make_async_copy(some, some, c_recv.at[kk]).wait()

    def dense_chunk(kk, carry):
        context_wait(kk)

        def columns(j, c):
            at = pl.ds(pl.multiple_of(j * DENSE_COLS, DENSE_COLS), DENSE_COLS)
            here = pl.ds(pl.multiple_of(kk * chunk, chunk), chunk)
            x = cr[pl.ds(kk * part, part)].reshape(chunk, width)
            dense = jnp.dot(x, wd_v[:, at], preferred_element_type=jnp.float32) + vecs[2:3, at]
            out_v[here, at] = (a_v[0, here, at].astype(jnp.float32) * ALPHA + dense).astype(jnp.bfloat16)
            return c

        lax.fori_loop(0, width // DENSE_COLS, columns, 0)
        return carry

    lax.fori_loop(0, CHUNKS - 1, dense_chunk, 0)
    rest_v[...] = a_v[0, pl.ds((CHUNKS - 1) * chunk, chunk), :].astype(jnp.float32) * ALPHA + vecs[2:3, :]
    for side in range(2):
        whole = a_v.at[0]
        pltpu.make_async_copy(whole, whole, a_send.at[side]).wait()
    pltpu.make_async_copy(fwd, fwd, f_send).wait()

    @pl.when(me == n - 1)
    def _():
        for step in range(1, n):
            pltpu.make_async_copy(pos_v, m_v, m_send.at[step]).wait()

    sent = cs.at[pl.ds(0, n - 1)]
    pltpu.make_async_copy(sent, sent, c_send).wait()
    context_wait(CHUNKS - 1)
    last_v[...] = cr[pl.ds((CHUNKS - 1) * part, part)].reshape(chunk, width)


def finish_kernel(out_v, k_v, v_v, wd_v, last_v, rest_v, out, k_out, v_out, tail_v, sem, tail_sem):
    done = out_v.shape[0]
    chunk, width = last_v.shape
    copies = [pltpu.make_async_copy(k_v, k_out, sem.at[0]), pltpu.make_async_copy(v_v, v_out, sem.at[1]),
              pltpu.make_async_copy(out_v, out.at[pl.ds(0, done)], sem.at[2])]
    for copy in copies:
        copy.start()
    for j in range(width // DENSE_COLS):
        at = pl.ds(j * DENSE_COLS, DENSE_COLS)
        dense = jnp.dot(last_v[...], wd_v[:, at], preferred_element_type=jnp.float32)
        tail_v[:, at] = (rest_v[:, at] + dense).astype(jnp.bfloat16)
        copy = pltpu.make_async_copy(tail_v.at[:, at], out.at[pl.ds(done, chunk), at], tail_sem.at[j])
        copy.start()
        copies.append(copy)
    for copy in copies:
        copy.wait()


def solution(mesh):
    n = mesh.shape['sp']
    seq_spec = P('dp', 'sp', None)
    row_spec = P('dp', 'sp')
    head_spec = P('dp', None, 'sp', None)
    replicated = P()

    def local_block(hidden, pos_ids, block_ids, ctx_len, ln_gamma, ln_beta, w_qkv, b_qkv, w_dense, b_dense):
        rows, toks, width = hidden.shape
        heads, _, dh = b_qkv.shape
        hl = heads // n
        seq = n * toks
        tokens = rows * toks
        part = rows // CHUNKS
        chunk = part * toks
        cols = 3 * hl * dh
        bf16, f32 = jnp.bfloat16, jnp.float32
        w_t = jnp.transpose(w_qkv, (1, 2, 3, 0)).reshape(n, hl, 3, dh, width)
        half = dh // 2
        inv_freq = ROPE_BASE ** (-np.arange(0, half, 2).astype(np.float32) / half)
        freq = np.tile(inv_freq.astype(np.float32), LANES // inv_freq.shape[0])[None, :]
        vmem = pl.BlockSpec(memory_space=pltpu.VMEM)
        anywhere = pl.BlockSpec(memory_space=pl.ANY)
        kv_shape = (rows, hl * dh, seq)
        staged = pl.pallas_call(
            functools.partial(block_kernel, n, rows, toks, dh),
            out_shape=[pltpu.VMEM((tokens - chunk, width), bf16), pltpu.VMEM(kv_shape, bf16), pltpu.VMEM(kv_shape, bf16),
                       pltpu.VMEM((width, width), bf16), pltpu.VMEM((chunk, width), bf16), pltpu.VMEM((chunk, width), f32)],
            in_specs=[anywhere] * 10,
            out_specs=[vmem] * 6,
            scratch_shapes=[
                pltpu.VMEM((12, 3, hl, dh, width), bf16),
                pltpu.VMEM((3, tokens, width), bf16),
                pltpu.VMEM((13, CHUNKS, part, toks, cols), bf16),
                pltpu.VMEM((rows, seq, cols), bf16),
                pltpu.VMEM((n, rows, toks, LANES), bf16),
                pltpu.VMEM((rows, toks, width), bf16),
                pltpu.VMEM((3, heads, dh), bf16),
                pltpu.VMEM((n, 1, cols), f32),
                pltpu.VMEM((width,), bf16),
                pltpu.VMEM((width,), bf16),
                pltpu.VMEM((width,), bf16),
                pltpu.VMEM((8, width), f32),
                pltpu.SMEM((rows,), jnp.int32),
                pltpu.VMEM((rows, toks), jnp.int32),
                pltpu.VMEM((rows, toks), jnp.int32),
                pltpu.VMEM((1, LANES), f32),
                pltpu.SemaphoreType.DMA((rows,)),
                pltpu.SemaphoreType.DMA((12,)),
                pltpu.SemaphoreType.DMA,
                pltpu.SemaphoreType.DMA((7,)),
                pltpu.SemaphoreType.DMA((2,)),
                pltpu.SemaphoreType.DMA((2, CHUNKS)),
                pltpu.SemaphoreType.DMA,
                pltpu.SemaphoreType.DMA((CHUNKS,)),
                pltpu.SemaphoreType.DMA,
                pltpu.SemaphoreType.DMA((CHUNKS,)),
                pltpu.SemaphoreType.DMA((n,)),
                pltpu.SemaphoreType.DMA,
            ],
            compiler_params=pltpu.CompilerParams(collective_id=0, has_side_effects=True, vmem_limit_bytes=46 * 2**20),
            name='attention_block',
        )(hidden.reshape(tokens, width), w_t, jnp.transpose(b_qkv, (1, 0, 2)), w_dense, ln_gamma, ln_beta, b_dense, ctx_len, pos_ids, freq)
        out, k_out, v_out = pl.pallas_call(
            finish_kernel,
            out_shape=[jax.ShapeDtypeStruct((tokens, width), bf16)] + [jax.ShapeDtypeStruct(kv_shape, bf16)] * 2,
            in_specs=[vmem] * 6,
            out_specs=[anywhere] * 3,
            scratch_shapes=[pltpu.VMEM((chunk, width), bf16), pltpu.SemaphoreType.DMA((3,)), pltpu.SemaphoreType.DMA((width // DENSE_COLS,))],
            compiler_params=pltpu.CompilerParams(vmem_limit_bytes=4 * 2**20),
            name='finish_block',
        )(*staged)

        def to_heads(x):
            return jnp.transpose(x.reshape(rows, hl, dh, seq), (0, 3, 1, 2))

        return out.reshape(rows, toks, width), to_heads(k_out), to_heads(v_out)

    return jax.shard_map(local_block, mesh=mesh, in_specs=(seq_spec, row_spec, row_spec, P('dp'), replicated, replicated, replicated, replicated, replicated, replicated), out_specs=(seq_spec, head_spec, head_spec), check_vma=False)
```

time: 203 us -> 182 us (0.90)
  local copies, waits for them, and re-layouts: 12.4 us -> 0 us
  Pallas kernels: 187 us -> 181 us
  other arithmetic: 2.29 us -> 0 us
    pallas_call x1, Pallas kernels: 187 us -> 178 us  [local_block(): pl.pallas_call(functools.partial(block_kernel, n, rows, toks, dh), out_sh...]
    unnamed x7 -> x0, local copies, waits for them, and re-layouts: 6.98 us -> none
    another operation x5 -> x0, local copies, waits for them, and re-layouts: 2.74 us -> none  [the longest x3 2.08 us: local_block(): vecs = jnp.stack([ln_gamma, ln_beta, b_dense]).astype(jnp.float32)]
    pallas_call x0 -> x1, Pallas kernels: none -> 2.69 us  [local_block(): pl.pallas_call(finish_kernel, out_shape=[jax.ShapeDtypeStruct((tokens, wi...]
where the time goes in v2:
time: 182 us
  Pallas kernels  181 us (99%)
    pallas_call x1, Pallas kernels, local_block(): pl.pallas_call(functools.partial(block_kernel, n, rows, toks, dh), out_sh...  178 us

profile of v2, /device:TPU:21, one launch (start us, length us, event | category | flops | bytes accessed | tf_op | source)
XLA Modules:
  0.0 181.8 jit_solution(6681111486479268075)
XLA Ops:
  0.6 178.4 %attention_block.1 = (bf16[384,2048]{1,0:T(8,128)(2,1)S(1)}, bf16[16,128,512]{2,1,0:T(8,128)(2,1)S(1)}, bf16[16,128,512]{2,1,0:T(8,128)(2,1)S(1)}, bf16[2048,204...) custom-call(bf16[512,2048]{1,0:T(8,128)(2,1)} %bitcast.13, ...), custom_call_target="tpu_custom_call" | custom-call | tf_op jit(solution)/shard_map/attention_block/pallas_call | solution.py:357
  179.1 2.7 %finish_block.1 = (bf16[512,2048]{1,0:T(8,128)(2,1)}, bf16[16,128,512]{2,1,0:T(8,128)(2,1)}, bf16[16,128,512]{2,1,0:T(8,128)(2,1)}) custom-call(bf16[384,2048]{1,0:T(8,128)(2,1)S(1)} %get-tuple-element.12.out_v, bf16[16,128,512]{2,1,0:T(8,128)(2,1)S(1)} %get-tuple-element.13.k_v, bf16[16,128,512]{2,1,0:T(8,128)(2,1)S(1)} %get-tuple-element.14.v_v, ...), custom_call_target="tpu_custom_call" | custom-call | tf_op jit(solution)/shard_map/finish_block/pallas_call | solution.py:396

commit v3 on v2

--- a/solution.py
+++ b/solution.py
@@ -19,6 +19,7 @@
 CTX_MIN = 128
 CTX_MAX = 384
 FIRST_ROWS = 4
+PLACES = 12
 DENSE_COLS = 512
 MESH = pl.DeviceIdType.MESH
 NT = (((1,), (1,)), ((), ()))
@@ -34,8 +35,8 @@
 
 def block_kernel(n, rows, toks, dh, hidden, w_hbm, bq_hbm, wd_hbm, gamma_hbm, beta_hbm, bd_hbm, ctx_hbm, pos_hbm, freq_hbm,
                  out_v, k_v, v_v, wd_v, last_v, rest_v,
-                 w_v, a_v, fwd, qkv, cs, cr, bq_v, bias, g_v, be_v, bd_v, vecs, ctx, pos_v, m_v, freq,
-                 h_sem, w_sem, wd_sem, small_sem, a_send, a_recv, f_send, q_recv, c_send, c_recv, m_send, m_recv):
+                 w_v, a_v, fwd, qkv, cs, cr, bq_v, bias, g_v, be_v, bd_v, vecs, ctx, pos_v, m_v, freq, table,
+                 h_sem, w_sem, wd_sem, small_sem, a_send, a_recv, r_send, r_recv, f_send, q_recv, c_send, c_recv, m_send, m_recv):
     me = lax.axis_index('sp')
     chips = n // CORES
     chip, core = me // CORES, me % CORES
@@ -85,23 +86,28 @@
         centered = x - mean
         var = jnp.mean(jnp.square(centered), axis=-1, keepdims=True)
         a_v[0, row_at(r), :] = (centered * lax.rsqrt(var + LN_EPS) * vecs[0:1, :] + vecs[1:2, :]).astype(jnp.bfloat16)
+        return carry
+
+    def norm_send_row(r, carry):
+        norm_row(r, carry)
         for side in range(2):
             a_copy(pl.multiple_of(r * toks, toks), toks, r // part, side).start()
         return carry
 
-    lax.fori_loop(0, FIRST_ROWS, norm_row, 0)
+    lax.fori_loop(0, FIRST_ROWS, norm_send_row, 0)
 
     def weight_copy(slot, block):
         for h in range(hl):
             for t in range(3):
                 pltpu.make_async_copy(w_hbm.at[block, h, t], w_v.at[slot, t, h], w_sem.at[slot]).start()
 
-    weight_blocks = [(0, 0), (0, 1), (1, 0), (1, 1), (2, 0), (2, 1), (-1, 0), (-1, 1), (-2, 0), (-2, 1), (3, 0), (-3, 1)]
+    weight_blocks = [(step, kore) for step in (0, 1, 2, -1, -2) for kore in range(CORES)]
     for slot, (step, kore) in enumerate(weight_blocks):
         weight_copy(slot, ((chip + step + chips) % chips) * CORES + kore)
     wd_copy = pltpu.make_async_copy(wd_hbm, wd_v, wd_sem)
     wd_copy.start()
-    lax.fori_loop(FIRST_ROWS, rows, norm_row, 0)
+    lax.fori_loop(FIRST_ROWS, 2 * part, norm_send_row, 0)
+    lax.fori_loop(2 * part, rows, norm_row, 0)
 
     for copy in small_copies[2:]:
         copy.wait()
@@ -134,63 +140,102 @@
         pltpu.make_async_remote_copy(src_ref=fwd.at[slot, k], dst_ref=qkv.at[at[0], at[1]], send_sem=f_send, recv_sem=q_recv.at[k],
                                      device_id=dest, device_id_type=MESH).start()
 
-    def to_own_chip(source, k, owner):
-        values = project(source, k, 0, CORES, chip * CORES)
+    def job(source, k, slot, target, owner, place, apart, own):
+        values = project(source, k, slot, CORES, target * CORES)
         for h in range(CORES):
-            @pl.when(core == h)
+            keep = jnp.logical_and(own == 1, core == h)
+
+            @pl.when(keep)
             def _():
                 at = owner_at(k, owner)
                 qkv[at[0], at[1], :] = values[h]
-                send(values[CORES - 1 - h], k, source, owner, device(chip, CORES - 1 - h))
+
+            @pl.when(jnp.logical_not(keep))
+            def _():
+                send(values[h], k, place + h * apart, owner, device(target, h))
 
     def wait_weights(slot):
         pltpu.make_async_copy(w_v.at[slot], w_v.at[slot], w_sem.at[slot]).wait()
 
+    table_rows = table.shape[1]
+
+    def table_block(i, carry):
+        at = pl.ds(pl.multiple_of(i * LANES, LANES), LANES)
+        index = lax.broadcasted_iota(jnp.int32, (LANES, LANES), 0) + (i * LANES - seq)
+        angle = jnp.maximum(index, 0).astype(jnp.float32) * freq[...]
+        quarter = lax.broadcasted_iota(jnp.int32, (LANES, LANES), 1) % (dh // 2) < dh // 4
+        sin = jnp.sin(angle)
+        table[0, at, :] = jnp.cos(angle)
+        table[1, at, :] = jnp.where(quarter, -sin, sin)
+        return carry
+
+    lax.fori_loop(0, table_rows // LANES, table_block, 0)
     for slot in range(CORES):
         wait_weights(slot)
 
+    def chip_at(offset):
+        return (chip + offset + chips) % chips
+
+    def chunk_at(k):
+        return pl.ds(pl.multiple_of(k * chunk, chunk), chunk)
+
     def own_chunk(k, carry):
-        to_own_chip(0, k, me)
+        job(0, k, 0, chip, me, 0, 0, 1)
+        return carry
+
+    def relay(k):
+        odd = k % 2
+        return pltpu.make_async_remote_copy(src_ref=a_v.at[1 + odd, chunk_at(k)], dst_ref=a_v.at[3, chunk_at(k)],
+                                            send_sem=r_send, recv_sem=r_recv.at[k],
+                                            device_id=device(chip_at(1 - 2 * odd), core), device_id_type=MESH)
+
+    def near_chunk(k, carry):
+        odd = k % 2
+        for side in range(2):
+            a_copy(pl.multiple_of(k * chunk, chunk), chunk, k, side).wait_recv()
+        relay(k).start()
+
+        def one(i, c):
+            own = i // 2
+            step = (2 - i) * (1 - own)
+            source = (1 - own) * (2 - odd) + own * ((3 - i) * (1 + odd) + (i - 2) * (2 - odd))
+            slot = (1 - own) * (CORES + CORES * (2 * (1 - odd) + step - 1))
+            place = (1 - own) * (4 + CORES * (step - 1)) + own * source
+            owner = chip_at(2 * source - 3) * CORES + core
+            job(source, k, slot, chip_at((2 * odd - 1) * step), owner, place, 1 - own, own)
+            return c
+
+        lax.fori_loop(0, 4, one, 0)
+        return carry
+
+    def far_chunk(k, carry):
+        odd = k % 2
+        there = a_v.at[3, chunk_at(k)]
+        pltpu.make_async_copy(there, there, r_recv.at[k]).wait()
+        owner = chip_at(4 * odd - 2) * CORES + core
+
+        def one(i, c):
+            own = i // 2
+            step = 2 - i
+            slot = (1 - own) * (CORES + CORES * (2 * odd + step - 1))
+            place = (1 - own) * (8 + CORES * (step - 1)) + own * 3
+            job(3, k, slot, chip_at((1 - 2 * odd) * step), owner, place, 1 - own, own)
+            return c
+
+        lax.fori_loop(0, 3, one, 0)
         return carry
 
     lax.fori_loop(0, CHUNKS, own_chunk, 0)
     for slot in range(CORES, len(weight_blocks)):
         wait_weights(slot)
-
-    def neighbour(side):
-        return ((chip - 1 + 2 * side + chips) % chips) * CORES + core
-
-    def forward_chunk(k, carry):
+    near_chunk(0, 0)
+    for k in range(2, CHUNKS):
         for side in range(2):
-            a_copy(pl.multiple_of(k * chunk, chunk), chunk, k, side).wait_recv()
-
-        def single(side, c):
-            owner = neighbour(side)
-            target = (chip + (1 - 2 * side) * 3 + chips) % chips
-            values = project(1 + side, k, 10 + side, 1, target * CORES + side)
-            send(values[0], k, 11 + side, owner, device(target, side))
-            return c
-
-        def pair(i, c):
-            side, step = i % 2, 2 - i // 2
-            index = 2 * side + step - 1
-            owner = neighbour(side)
-            target = (chip + (1 - 2 * side) * step + chips) % chips
-            values = project(1 + side, k, CORES + CORES * index, CORES, target * CORES)
-            for h in range(CORES):
-                send(values[h], k, 3 + CORES * index + h, owner, device(target, h))
-            return c
-
-        def own(side, c):
-            to_own_chip(1 + side, k, neighbour(side))
-            return c
-
-        lax.fori_loop(0, 2, single, 0)
-        lax.fori_loop(0, 4, pair, 0)
-        lax.fori_loop(0, 2, own, 0)
-        return carry
-
-    lax.fori_loop(0, CHUNKS, forward_chunk, 0)
+            a_copy(k * chunk, chunk, k, side).start()
+    near_chunk(1, 0)
+    far_chunk(0, 0)
+    lax.fori_loop(2, CHUNKS, near_chunk, 0)
+    far_chunk(1, 0)
 
     @pl.when(me != n - 1)
     def _():
@@ -207,12 +252,11 @@
         ctx_b = ctx[b]
         m_b = jnp.sum(jnp.where(last_lane, m_v[pl.ds(b, 1), :].astype(jnp.float32), 0.0), axis=-1, keepdims=True)
         in_ctx = row_iota < ctx_b
-        pos = jnp.where(in_ctx, row_iota.astype(jnp.float32), m_b)
-        blk = jnp.where(in_ctx, 0, row_iota - ctx_b + 1).astype(jnp.float32)
-        angle = jnp.where(by_pos, pos, blk) * freq[...]
-        cos = jnp.cos(angle)
-        sin = jnp.sin(angle)
-        sin = jnp.where(pair_low, -sin, sin)
+        angle_m = m_b * freq[...]
+        sin_m = jnp.sin(angle_m)
+        sin_m = jnp.where(pair_low[0:1], -sin_m, sin_m)
+        cos, sin = [jnp.where(by_pos, jnp.where(in_ctx, table[i, seq:2 * seq, :], trig_m), table[i, pl.ds(seq + 1 - ctx_b, seq), :])
+                    for i, trig_m in enumerate([jnp.cos(angle_m), sin_m])]
 
         def rotate(x):
             swapped = jnp.where(pair_low, pltpu.roll(x, LANES - dh // 4, 1), pltpu.roll(x, dh // 4, 1))
@@ -256,7 +300,7 @@
             cs[pl.ds(qt * owners, owners), b] = total.astype(jnp.bfloat16).reshape(owners, toks, LANES)
 
     def attend_chunk(kk, carry):
-        some = qkv.at[pl.ds(kk * part, part), pl.ds(0, 13 * toks)]
+        some = qkv.at[pl.ds(kk * part, part), pl.ds(0, PLACES * toks)]
         pltpu.make_async_copy(some, some, q_recv.at[kk]).wait()
 
         def one_row(r, c):
@@ -273,7 +317,9 @@
         cr[rows_k, :, cols_me] = cs[me, rows_k]
         return carry
 
-    lax.fori_loop(0, CHUNKS, attend_chunk, 0)
+    attend_chunk(0, 0)
+    lax.fori_loop(2, CHUNKS, far_chunk, 0)
+    lax.fori_loop(1, CHUNKS, attend_chunk, 0)
     wd_copy.wait()
 
     def context_wait(kk):
@@ -300,6 +346,7 @@
         whole = a_v.at[0]
         pltpu.make_async_copy(whole, whole, a_send.at[side]).wait()
     pltpu.make_async_copy(fwd, fwd, f_send).wait()
+    pltpu.make_async_copy(a_v.at[3], a_v.at[3], r_send).wait()
 
     @pl.when(me == n - 1)
     def _():
@@ -361,9 +408,9 @@
             in_specs=[anywhere] * 10,
             out_specs=[vmem] * 6,
             scratch_shapes=[
-                pltpu.VMEM((12, 3, hl, dh, width), bf16),
-                pltpu.VMEM((3, tokens, width), bf16),
-                pltpu.VMEM((13, CHUNKS, part, toks, cols), bf16),
+                pltpu.VMEM((10, 3, hl, dh, width), bf16),
+                pltpu.VMEM((4, tokens, width), bf16),
+                pltpu.VMEM((PLACES, CHUNKS, part, toks, cols), bf16),
                 pltpu.VMEM((rows, seq, cols), bf16),
                 pltpu.VMEM((n, rows, toks, LANES), bf16),
                 pltpu.VMEM((rows, toks, width), bf16),
@@ -377,12 +424,15 @@
                 pltpu.VMEM((rows, toks), jnp.int32),
                 pltpu.VMEM((rows, toks), jnp.int32),
                 pltpu.VMEM((1, LANES), f32),
+                pltpu.VMEM((2, 2 * seq + LANES, LANES), f32),
                 pltpu.SemaphoreType.DMA((rows,)),
-                pltpu.SemaphoreType.DMA((12,)),
+                pltpu.SemaphoreType.DMA((10,)),
                 pltpu.SemaphoreType.DMA,
                 pltpu.SemaphoreType.DMA((7,)),
                 pltpu.SemaphoreType.DMA((2,)),
                 pltpu.SemaphoreType.DMA((2, CHUNKS)),
+                pltpu.SemaphoreType.DMA,
+                pltpu.SemaphoreType.DMA((CHUNKS,)),
                 pltpu.SemaphoreType.DMA,
                 pltpu.SemaphoreType.DMA((CHUNKS,)),
                 pltpu.SemaphoreType.DMA,

time: 182 us -> 179 us (0.984)
  Pallas kernels: 181 us -> 178 us
    pallas_call x1, Pallas kernels: 178 us -> 175 us  [local_block(): pl.pallas_call(functools.partial(block_kernel, n, rows, toks, dh), out_sh...]
where the time goes in v3:
time: 179 us
  Pallas kernels  178 us (99%)
    pallas_call x1, Pallas kernels, local_block(): pl.pallas_call(functools.partial(block_kernel, n, rows, toks, dh), out_sh...  175 us

profile of v3, /device:TPU:21, one launch (start us, length us, event | category | flops | bytes accessed | tf_op | source)
XLA Modules:
  0.0 178.8 jit_solution(1846198233585714379)
XLA Ops:
  0.6 175.5 %attention_block.1 = (bf16[384,2048]{1,0:T(8,128)(2,1)S(1)}, bf16[16,128,512]{2,1,0:T(8,128)(2,1)S(1)}, bf16[16,128,512]{2,1,0:T(8,128)(2,1)S(1)}, bf16[2048,204...) custom-call(bf16[512,2048]{1,0:T(8,128)(2,1)} %bitcast.13, ...), custom_call_target="tpu_custom_call" | custom-call | tf_op jit(solution)/shard_map/attention_block/pallas_call | solution.py:404
  176.1 2.7 %finish_block.1 = (bf16[512,2048]{1,0:T(8,128)(2,1)}, bf16[16,128,512]{2,1,0:T(8,128)(2,1)}, bf16[16,128,512]{2,1,0:T(8,128)(2,1)}) custom-call(bf16[384,2048]{1,0:T(8,128)(2,1)S(1)} %get-tuple-element.12.out_v, bf16[16,128,512]{2,1,0:T(8,128)(2,1)S(1)} %get-tuple-element.13.k_v, bf16[16,128,512]{2,1,0:T(8,128)(2,1)S(1)} %get-tuple-element.14.v_v, ...), custom_call_target="tpu_custom_call" | custom-call | tf_op jit(solution)/shard_map/finish_block/pallas_call | solution.py:446

commit v4 on v3

--- a/solution.py
+++ b/solution.py
@@ -61,16 +61,16 @@
 
     small = [(gamma_hbm, g_v), (beta_hbm, be_v), (bd_hbm, bd_v), (bq_hbm, bq_v), (ctx_hbm, ctx), (pos_hbm, pos_v), (freq_hbm, freq)]
     small_copies = [pltpu.make_async_copy(src, dst, small_sem.at[i]) for i, (src, dst) in enumerate(small)]
+    hidden_copy(0).start()
     for copy in small_copies[:2]:
         copy.start()
-    for r in range(rows):
+    for r in range(1, rows):
         hidden_copy(r).start()
     for copy in small_copies[2:]:
         copy.start()
     for i in range(2):
         small_copies[i].wait()
         vecs[i:i + 1, :] = small[i][1][...].astype(jnp.float32)[None, :]
-    pl.semaphore_wait(barrier, n - 1)
 
     def a_copy(start, size, k, side):
         peer = device(chip + 1 - 2 * side + chips, core)
@@ -88,13 +88,19 @@
         a_v[0, row_at(r), :] = (centered * lax.rsqrt(var + LN_EPS) * vecs[0:1, :] + vecs[1:2, :]).astype(jnp.bfloat16)
         return carry
 
+    def send_row(r):
+        for side in range(2):
+            a_copy(pl.multiple_of(r * toks, toks), toks, r // part, side).start()
+
     def norm_send_row(r, carry):
         norm_row(r, carry)
-        for side in range(2):
-            a_copy(pl.multiple_of(r * toks, toks), toks, r // part, side).start()
-        return carry
-
-    lax.fori_loop(0, FIRST_ROWS, norm_send_row, 0)
+        send_row(r)
+        return carry
+
+    norm_row(0, 0)
+    pl.semaphore_wait(barrier, n - 1)
+    send_row(0)
+    lax.fori_loop(1, FIRST_ROWS, norm_send_row, 0)
 
     def weight_copy(slot, block):
         for h in range(hl):

time: 179 us -> 177 us (0.989)
  no operation moved by 1% of the time
where the time goes in v4:
time: 177 us
  Pallas kernels  177 us (100%)
    pallas_call x1, Pallas kernels, local_block(): pl.pallas_call(functools.partial(block_kernel, n, rows, toks, dh), out_sh...  174 us

profile of v4, /device:TPU:21, one launch (start us, length us, event | category | flops | bytes accessed | tf_op | source)
XLA Modules:
  0.0 177.4 jit_solution(16532791999485842985)
XLA Ops:
  0.6 174.1 %attention_block.1 = (bf16[384,2048]{1,0:T(8,128)(2,1)S(1)}, bf16[16,128,512]{2,1,0:T(8,128)(2,1)S(1)}, bf16[16,128,512]{2,1,0:T(8,128)(2,1)S(1)}, bf16[2048,204...) custom-call(bf16[512,2048]{1,0:T(8,128)(2,1)} %bitcast.13, ...), custom_call_target="tpu_custom_call" | custom-call | tf_op jit(solution)/shard_map/attention_block/pallas_call | solution.py:410
  174.7 2.7 %finish_block.1 = (bf16[512,2048]{1,0:T(8,128)(2,1)}, bf16[16,128,512]{2,1,0:T(8,128)(2,1)}, bf16[16,128,512]{2,1,0:T(8,128)(2,1)}) custom-call(bf16[384,2048]{1,0:T(8,128)(2,1)S(1)} %get-tuple-element.12.out_v, bf16[16,128,512]{2,1,0:T(8,128)(2,1)S(1)} %get-tuple-element.13.k_v, bf16[16,128,512]{2,1,0:T(8,128)(2,1)S(1)} %get-tuple-element.14.v_v, ...), custom_call_target="tpu_custom_call" | custom-call | tf_op jit(solution)/shard_map/finish_block/pallas_call | solution.py:452
